TPU v7x, 32 devices: a whole 2x2x4 slice. The times are simulated.
32 devices in a mesh: dp: 2 (over x), rep: 4 (over y, core), ind: 4 (over z).
Axes of the slice: x: 2, y: 2, z: 4, core: 2. Of those that a mesh axis runs over, the one named last changes fastest.
Arguments:
- points: bfloat16 [6144, 64], P(('dp', 'rep')), may hold values from -6 to 6
- targets: float32 [6144], P(('dp', 'rep')), may hold values from -6 to 6
- inducing: float32 [4096, 64], P('ind'), may hold values from -6 to 6
- whitening: bfloat16 [4096, 4096], P('ind'), may hold values from -0.0546875 to 0.0546875
- mean_v: float32 [4096], P('ind'), may hold values from -12 to 12
- covariance: float32 [4096, 4096], P('ind', ('dp', 'rep')), may hold values from -24 to 24
- precision: float32 [4096, 4096], P('ind', ('dp', 'rep')), may hold values from -3 to 3
- natural_one: float32 [4096], P('ind'), may hold values from -6 to 6
- lengthscales: float32 [64], replicated, may hold values from 1.6 to 24
- hypers: float32 [2], replicated, may hold values from 0.5 to 2
Outputs:
- precision_new: float32 [4096, 4096], P('ind', ('dp', 'rep'))
- natural_new: float32 [4096], P('ind')
- expected_fit: float32 [], replicated
All inputs are finite; a program needn't handle non-finite values.
Results may differ from a plain program's by a relative error of at most 0.0076.
Values may be sent and summed in bfloat16 or wider, within the bound.
A program may use at most 128 MiB of HBM per device.

v0:
```python
import jax
import jax.numpy as jnp
from jax import lax
from jax.sharding import PartitionSpec as P


def cross_cov(inducing, points, lengthscales, signal):
    scaled_z = inducing / lengthscales
    scaled_x = points.astype(jnp.float32) / lengthscales
    norm_z = jnp.sum(scaled_z * scaled_z, axis=1)
    norm_x = jnp.sum(scaled_x * scaled_x, axis=1)
    inner = jnp.dot(scaled_z, scaled_x.T, precision=lax.Precision.HIGHEST)
    return (signal * jnp.exp(-0.5 * (norm_z[:, None] + norm_x[None, :] - 2.0 * inner))).astype(
        jnp.bfloat16
    )


def shards(
    points,
    targets,
    inducing,
    whitening,
    mean_v,
    covariance,
    precision,
    natural_one,
    lengthscales,
    hypers,
):
    signal = hypers[0]
    noise_var = hypers[1]
    all_inducing = lax.all_gather(inducing, "ind", axis=0, tiled=True)
    cross = cross_cov(all_inducing, points, lengthscales, signal)
    white = jnp.dot(whitening, cross, preferred_element_type=jnp.float32).astype(jnp.bfloat16)
    white_wide = white.astype(jnp.float32)
    mean_part = jnp.dot(mean_v, white_wide, precision=lax.Precision.HIGHEST)
    square_part = jnp.sum(white_wide * white_wide, axis=0)
    gram_part = lax.dot_general(
        white,
        lax.all_gather(white, "ind", axis=0, tiled=True),
        (((1,), (1,)), ((), ())),
        preferred_element_type=jnp.float32,
    )
    pred_mean, sq_norm = lax.psum((mean_part, square_part), "ind")
    resid = targets - pred_mean
    local_fit = jnp.sum(resid * resid + signal - sq_norm)
    local_proj = jnp.dot(white_wide, targets, precision=lax.Precision.HIGHEST)
    proj, fit_sum = lax.psum((local_proj, local_fit), ("dp", "rep"))
    own_rows = gram_part.shape[0]
    gram = lax.psum_scatter(gram_part, ("dp", "rep"), scatter_dimension=1, tiled=True)
    own_cols = gram.shape[1]
    trace = lax.psum(jnp.sum(covariance * gram), ("dp", "rep", "ind"))
    total = points.shape[0] * lax.axis_size(("dp", "rep"))
    expected_fit = -0.5 * jnp.log(2.0 * jnp.pi * noise_var) - (fit_sum + trace) / (
        2.0 * noise_var * total
    )
    row_ids = lax.axis_index("ind") * own_rows + jnp.arange(own_rows, dtype=jnp.int32)
    col_ids = lax.axis_index(("dp", "rep")) * own_cols + jnp.arange(own_cols, dtype=jnp.int32)
    identity = (row_ids[:, None] == col_ids[None, :]).astype(jnp.float32)
    precision_new = 0.5 * precision + 0.5 * (identity + gram / noise_var)
    natural_new = 0.5 * natural_one + 0.5 * proj / noise_var
    return (precision_new, natural_new, expected_fit)


def solution(mesh):
    return jax.shard_map(
        shards,
        mesh=mesh,
        in_specs=(
            P(("dp", "rep"), None),
            P(("dp", "rep")),
            P("ind", None),
            P("ind", None),
            P("ind"),
            P("ind", ("dp", "rep")),
            P("ind", ("dp", "rep")),
            P("ind"),
            P(),
            P(),
        ),
        out_specs=(P("ind", ("dp", "rep")), P("ind"), P()),
        check_vma=False,
    )
```

profile of v0, /device:TPU:0, one launch (start us, length us, event | category | flops | bytes accessed | tf_op | source)
XLA Modules:
  0.0 361.2 jit_solution(7977664895981380709)
XLA Ops:
  7.2 0.0 copy-start
  7.2 0.0 all-gather.3.cloned.1.call-start
  7.2 0.7 all-gather.3.cloned.1.call-update
  7.9 0.0 all-gather.5.cloned.1.call-start
  8.0 1.3 fusion.4
  9.3 1.0 multiply_reduce_fusion.3
  10.3 30.0 %all-gather.3.cloned.1.call-done = f32[4096,64]{0,1:T(8,128)} async-done(((f32[1024,64]{0,1:T(8,128)}), f32[4096,64]{0,1:T(8,128)}) %all-gather.3.cloned.1.call-update) | async-done | bytes 1048592 | tf_op jit(solution)/shard_map/all_gather | solution.py:32
  40.3 0.0 slice-start
  40.3 1.6 multiply_reduce_fusion.2
  41.9 0.0 slice-start.1
  41.9 14.8 %multiply_convert_fusion = bf16[4096,768]{1,0:T(8,128)(2,1)S(1)} fusion(f32[768]{0:T(1024)S(1)} %multiply_reduce_fusion.3, f32[4096]{0:T(1024)S(1)} %multiply_reduce_fusion.2, f32[]{:T(128)} %bitcast, f32[4096,64]{0,1:T(8,128)} %all-gather.3.cloned.1.call-done, f32[64]{0:T(128)} %param.18, bf16[768,64]{0,1:T(8,128)(2,1)} %param.10), kind=kOutput, calls=%fused_computation | convolution fusion | flops 2435153920 | bytes 7458052 | tf_op jit(solution)/shard_map/dot_general | solution.py:12
  56.7 0.0 slice-done
  56.7 0.0 slice-done.1
  56.7 7.9 %multiply_reduce_fusion = (f32[768]{0:T(1024)S(1)}, bf16[768,1024]{1,0:T(8,128)(2,1)}) fusion(bf16[4096,768]{1,0:T(8,128)(2,1)S(1)} %multiply_convert_fusion, bf16[1024,4096]{1,0:T(8,128)(2,1)S(1)} %bitcast.20), kind=kOutput, calls=%fused_computation.1 | convolution fusion | flops 6445595648 | bytes 16256000 | tf_op jit(solution)/shard_map/dot_general | solution.py:34
  64.6 0.0 all-gather.5.cloned.1.call-update
  64.6 0.2 reduce-scatter.2.cloned.1.call-start
  64.8 114.6 %all-gather.5.cloned.1.call-done = bf16[4096,768]{0,1:T(8,128)(2,1)} async-done(((bf16[1024,768]{0,1:T(8,128)(2,1)}), bf16[4096,768]{0,1:T(8,128)(2,1)}) %all-gather.5.cloned.1.call-update) | async-done | bytes 6291472 | tf_op jit(solution)/shard_map/all_gather | solution.py:40
  179.5 12.5 %fusion.5 = f32[1024,4096]{1,0:T(8,128)} fusion(bf16[768,1024]{1,0:T(8,128)(2,1)} %get-tuple-element.12, bf16[4096,768]{0,1:T(8,128)(2,1)} %all-gather.5.cloned.1.call-done), kind=kOutput, calls=%fused_computation.19 | convolution fusion | flops 6442450944 | bytes 24641536 | tf_op jit(solution)/shard_map/dot_general | solution.py:38
  192.0 0.0 copy-start.2
  192.0 0.0 copy-start.1
  192.0 0.0 reduce-scatter.2.cloned.1.call-update
  192.0 0.0 copy-start.3
  192.1 0.6 copy-done.2
  194.1 0.0 copy-done
  194.1 0.0 copy-done.1
  194.1 1.3 convolution_reduce_fusion
  195.4 8.8 %all-reduce.1 = (f32[768]{0:T(1024)S(1)}, f32[768]{0:T(1024)S(1)}) all-reduce(f32[768]{0:T(1024)S(1)} %get-tuple-element.11, f32[768]{0:T(1024)S(1)} %convolution_reduce_fusion), channel_id=1, replica_groups=mesh['dp'=2,'rep'=4,'ind'=4] {'ind'}, use_global_device_ids=true, to_apply=%region_6.0 | all-reduce | flops 1536 | bytes 12288 | tf_op jit(solution)/shard_map/psum | solution.py:44
  204.2 1.3 subtract_reduce_fusion
  205.5 0.7 fusion.2
  206.2 12.9 %all-reduce = (f32[1024]{0:T(1024)S(1)}, f32[]{:T(128)}) all-reduce(f32[1024]{0:T(1024)S(1)} %bitcast.18, f32[]{:T(128)} %subtract_reduce_fusion), channel_id=1, replica_groups=mesh['dp'=2,'rep'=4,'ind'=4] {'dp','rep'}, use_global_device_ids=true, to_apply=%region_3.0 | all-reduce | flops 1025 | bytes 8200 | tf_op jit(solution)/shard_map/psum | solution.py:48
  219.2 0.0 copy-done.3
  219.2 1.2 divide_add_fusion
  220.4 86.0 %reduce-scatter.2.cloned.1.call-done = f32[1024,512]{1,0:T(8,128)} async-done(((f32[1024,4096]{1,0:T(8,128)}), f32[1024,512]{1,0:T(8,128)}) %reduce-scatter.2.cloned.1.call-update) | async-done | bytes 2097168 | tf_op jit(solution)/shard_map/reduce_scatter | solution.py:50
  306.4 6.4 %multiply_reduce_fusion.1 = (f32[]{:T(128)}, f32[1024,512]{1,0:T(8,128)}) fusion(f32[1024,512]{1,0:T(8,128)} %param.15, f32[1024,512]{1,0:T(8,128)} %reduce-scatter.2.cloned.1.call-done, f32[1024,512]{1,0:T(8,128)} %param.16, f32[]{:T(128)} %bitcast.2, s32[512]{0:T(512)S(1)} %iota_add_fusion.1, s32[1024]{0:T(1024)S(1)} %iota_add_fusion), kind=kLoop, calls=%fused_computation.2 | loop fusion | flops 4194303 | bytes 8394760 | tf_op jit(solution)/shard_map/reduce_sum | solution.py:52
  312.8 39.5 %psum.39 = f32[]{:T(128)} all-reduce(f32[]{:T(128)} %get-tuple-element.7), channel_id=1, replica_groups=mesh['dp'=2,'rep'=4,'ind'=4] {'dp','rep','ind'}, use_global_device_ids=true, to_apply=%region_10.0 | all-reduce | flops 1 | bytes 8 | tf_op jit(solution)/shard_map/psum | solution.py:52
  (4 shorter events, 0.0 us)
Async XLA Ops:
  7.2 186.9 %copy-start = (f32[1024]{0:T(1024)S(1)}, f32[1024]{0:T(1024)}, u32[]{:S(2)}) copy-start(f32[1024]{0:T(1024)} %param.14) | copy-start | bytes 12292
  7.2 33.1 %all-gather.3.cloned.1.call-start = ((), (), s32[]{:S(2)}) async-start(), calls=%async_computation.1 | async-start | bytes 1310720 | tf_op jit(solution)/shard_map/all_gather | solution.py:32
  7.9 171.6 %all-gather.5.cloned.1.call-start = ((), (), s32[]{:S(2)}) async-start(), calls=%async_computation.2 | async-start | bytes 7864320 | tf_op jit(solution)/shard_map/all_gather | solution.py:40
  40.3 16.4 %slice-start = ((s8[8388608]{0:T(1024)(128)(4,1)}), s8[4194304]{0:T(1024)(128)(4,1)S(1)}, s32[]{:S(2)}) async-start(s8[8388608]{0:T(1024)(128)(4,1)} %bitcast.19), calls=%async_computation.4 | async-start | bytes 8388608
  41.9 14.8 %slice-start.1 = ((s8[8388608]{0:T(1024)(128)(4,1)}), s8[4194304]{0:T(1024)(128)(4,1)S(1)}, s32[]{:S(2)}) async-start(s8[8388608]{0:T(1024)(128)(4,1)} %bitcast.19), calls=%async_computation.5 | async-start | bytes 8388608
  64.6 241.8 %reduce-scatter.2.cloned.1.call-start = ((), (), s32[]{:S(2)}) async-start(), calls=%async_computation.3 | async-start | bytes 18874368 | tf_op jit(solution)/shard_map/reduce_scatter | solution.py:50
  192.0 0.7 copy-start.2
  192.0 2.1 copy-start.1
  192.0 27.1 %copy-start.3 = (f32[1024]{0:T(1024)S(1)}, f32[1024]{0:T(1024)}, u32[]{:S(2)}) copy-start(f32[1024]{0:T(1024)} %param.17) | copy-start | bytes 12292
Sparse Core Ops, SparseCore 0:
  9.6 30.6 all-gather.2
  64.7 114.6 all-gather.4
  192.2 114.2 reduce-scatter.1
where the time goes:
time: 362 us; the launch traced here: 361 us
  waiting for transfers between devices  231 us (64%)
  blocking collectives  61.2 us (17%)
  matrix products  37.2 us (10%)
  between operations  17.6 us (5%)
  other arithmetic  11.5 us (3%)
    all_gather x1, waiting for transfers between devices, shards(): lax.all_gather(white, 'ind', axis=0, tiled=True)  115 us
    reduce_scatter x1, waiting for transfers between devices, shards(): lax.psum_scatter(gram_part, ('dp', 'rep'), scatter_dimension=1, tiled=True)  86 us
    psum x1, blocking collectives, shards(): trace = lax.psum(jnp.sum(covariance * gram), ('dp', 'rep', 'ind'))  39.5 us
    all_gather x1, waiting for transfers between devices, shards(): all_inducing = lax.all_gather(inducing, 'ind', axis=0, tiled=True)  30 us
    dot_general x1, matrix products, cross_cov(): inner = jnp.dot(scaled_z, scaled_x.T, precision=lax.Precision.HIGHEST)  14.8 us
    psum x1, blocking collectives, shards(): proj, fit_sum = lax.psum((local_proj, local_fit), ('dp', 'rep'))  12.9 us
    dot_general x1, matrix products, shards(): lax.dot_general(white, lax.all_gather(white, 'ind', axis=0, tiled=True),...  12.5 us
    psum x1, blocking collectives, shards(): pred_mean, sq_norm = lax.psum((mean_part, square_part), 'ind')  8.8 us
  transfers between devices with their start and end apart: 3, of which 3 were waited for; matrix products, arithmetic and copies ran while one was open for 2% of the time, Pallas kernels for 0%

commit v1 on v0

--- a/solution.py
+++ b/solution.py
@@ -29,7 +29,12 @@
 ):
     signal = hypers[0]
     noise_var = hypers[1]
-    all_inducing = lax.all_gather(inducing, "ind", axis=0, tiled=True)
+    ring = [inducing]
+    for hop in range(3):
+        ring.append(lax.ppermute(ring[-1], "ind", [(dev, (dev + 1) % 4) for dev in range(4)]))
+    all_inducing = jnp.roll(
+        jnp.concatenate(ring[::-1], axis=0), (lax.axis_index("ind") + 1) * ring[0].shape[0], axis=0
+    )
     cross = cross_cov(all_inducing, points, lengthscales, signal)
     white = jnp.dot(whitening, cross, preferred_element_type=jnp.float32).astype(jnp.bfloat16)
     white_wide = white.astype(jnp.float32)

time: 362 us -> 356 us (0.983)
  waiting for transfers between devices: 231 us -> 223 us
    all_gather x1 -> x0, waiting for transfers between devices: 30 us -> none  [shards(): all_inducing = lax.all_gather(inducing, 'ind', axis=0, tiled=True)]
    ppermute x0 -> x3, waiting for transfers between devices: none -> 23.9 us  [shards(): lax.ppermute(ring[-1], 'ind', [(dev, (dev + 1) % 4) for dev in range(4)])]
  transfers between devices with their start and end apart: 3 -> 5, of which waited for: 3 -> 5; matrix products, arithmetic and copies ran while one was open for 2% -> 2% of each run, Pallas kernels for 0% -> 0%
where the time goes in v1:
time: 356 us; the launch traced here: 355 us
  waiting for transfers between devices  223 us (63%)
  blocking collectives  61.2 us (17%)
  matrix products  36.6 us (10%)
  between operations  18 us (5%)
  other arithmetic  10.1 us (3%)
    all_gather x1, waiting for transfers between devices, shards(): lax.all_gather(white, 'ind', axis=0, tiled=True)  113 us
    reduce_scatter x1, waiting for transfers between devices, shards(): lax.psum_scatter(gram_part, ('dp', 'rep'), scatter_dimension=1, tiled=True)  86 us
    psum x1, blocking collectives, shards(): trace = lax.psum(jnp.sum(covariance * gram), ('dp', 'rep', 'ind'))  39.5 us
    ppermute x3, waiting for transfers between devices, shards(): lax.ppermute(ring[-1], 'ind', [(dev, (dev + 1) % 4) for dev in range(4)])  23.9 us
    dot_general x1, matrix products, cross_cov(): inner = jnp.dot(scaled_z, scaled_x.T, precision=lax.Precision.HIGHEST)  13.6 us
    dot_general x1, matrix products, shards(): lax.dot_general(white, lax.all_gather(white, 'ind', axis=0, tiled=True),...  13 us
    psum x1, blocking collectives, shards(): proj, fit_sum = lax.psum((local_proj, local_fit), ('dp', 'rep'))  12.9 us
    psum x1, blocking collectives, shards(): pred_mean, sq_norm = lax.psum((mean_part, square_part), 'ind')  8.8 us
  transfers between devices with their start and end apart: 5, of which 5 were waited for; matrix products, arithmetic and copies ran while one was open for 2% of the time, Pallas kernels for 0%

profile of v1, /device:TPU:0, one launch (start us, length us, event | category | flops | bytes accessed | tf_op | source)
XLA Modules:
  0.0 355.5 jit_solution(691654738651894634)
XLA Ops:
  7.2 0.0 copy-start
  7.2 0.0 copy-start.2
  7.2 0.0 all-gather.2.cloned.1.call-start
  7.2 3.1 collective-permute-start
  10.3 8.5 %collective-permute-done = f32[1024,64]{0,1:T(8,128)S(1)} collective-permute-done((f32[1024,64]{0,1:T(8,128)}, f32[1024,64]{0,1:T(8,128)S(1)}, u32[]{:S(2)}, u32[]{:S(2)}) %collective-permute-start) | collective-permute-done | bytes 262176 | tf_op jit(solution)/shard_map/ppermute | solution.py:34
  18.9 0.0 collective-permute-start.1
  18.9 9.3 %collective-permute-done.1 = f32[1024,64]{0,1:T(8,128)S(1)} collective-permute-done((f32[1024,64]{0,1:T(8,128)S(1)}, f32[1024,64]{0,1:T(8,128)S(1)}, u32[]{:S(2)}, u32[]{:S(2)}) %collective-permute-start.1) | collective-permute-done | bytes 262176 | tf_op jit(solution)/shard_map/ppermute | solution.py:34
  28.2 0.0 collective-permute-start.2
  28.2 1.3 fusion.5
  29.5 1.0 multiply_reduce_fusion.3
  30.5 0.0 copy-start.6
  30.5 6.1 %collective-permute-done.2 = f32[1024,64]{0,1:T(8,128)S(1)} collective-permute-done((f32[1024,64]{0,1:T(8,128)S(1)}, f32[1024,64]{0,1:T(8,128)S(1)}, u32[]{:S(2)}, u32[]{:S(2)}) %collective-permute-start.2) | collective-permute-done | bytes 262176 | tf_op jit(solution)/shard_map/ppermute | solution.py:34
  36.6 0.0 copy-start.3
  36.7 1.0 constant_dynamic-update-slice_fusion.4
  37.7 0.0 copy-done.2
  37.8 0.0 copy-done.6
  37.8 0.0 slice-start
  37.8 0.2 multiply_reduce_fusion.2
  38.0 0.0 copy-done.3
  38.0 0.0 slice-start.1
  38.0 13.6 %multiply_convert_fusion = bf16[4096,768]{1,0:T(8,128)(2,1)S(1)} fusion(f32[768]{0:T(1024)S(1)} %multiply_reduce_fusion.3, f32[4096]{0:T(1024)S(1)} %multiply_reduce_fusion.2, f32[]{:T(128)} %bitcast, bf16[768,64]{0,1:T(8,128)(2,1)S(1)} %copy-done.3, f32[8192,64]{0,1:T(8,128)S(1)} %constant_dynamic-update-slice_fusion, s32[]{:T(128)S(6)} %select_n.14, ...), kind=kOutput, calls=%fused_computation | convolution fusion | flops 2435153920 | bytes 7459848 | tf_op jit(solution)/shard_map/dot_general | solution.py:12
  51.6 0.0 slice-done
  51.7 0.0 slice-done.1
  51.7 7.9 %multiply_reduce_fusion = (f32[768]{0:T(1024)S(1)}, bf16[768,1024]{1,0:T(8,128)(2,1)}) fusion(bf16[4096,768]{1,0:T(8,128)(2,1)S(1)} %multiply_convert_fusion, bf16[1024,4096]{1,0:T(8,128)(2,1)S(1)} %bitcast.20), kind=kOutput, calls=%fused_computation.1 | convolution fusion | flops 6445595648 | bytes 16256000 | tf_op jit(solution)/shard_map/dot_general | solution.py:39
  59.5 0.0 copy-start.1
  59.5 0.0 all-gather.2.cloned.1.call-update
  59.6 0.2 reduce-scatter.2.cloned.1.call-start
  59.8 113.0 %all-gather.2.cloned.1.call-done = bf16[4096,768]{0,1:T(8,128)(2,1)} async-done(((bf16[1024,768]{0,1:T(8,128)(2,1)}), bf16[4096,768]{0,1:T(8,128)(2,1)}) %all-gather.2.cloned.1.call-update) | async-done | bytes 6291472 | tf_op jit(solution)/shard_map/all_gather | solution.py:45
  172.8 0.0 copy-done.1
  172.8 13.0 %fusion.6 = f32[1024,4096]{1,0:T(8,128)} fusion(bf16[768,1024]{1,0:T(8,128)(2,1)S(1)} %copy-done.1, bf16[4096,768]{0,1:T(8,128)(2,1)} %all-gather.2.cloned.1.call-done), kind=kOutput, calls=%fused_computation.28 | convolution fusion | flops 6442450944 | bytes 24641536 | tf_op jit(solution)/shard_map/dot_general | solution.py:43
  185.9 0.0 copy-start.4
  185.9 0.0 reduce-scatter.2.cloned.1.call-update
  185.9 0.0 copy-start.5
  185.9 0.6 copy-done.4
  187.9 0.0 copy-done
  187.9 1.3 convolution_reduce_fusion
  189.3 8.8 %all-reduce.1 = (f32[768]{0:T(1024)S(1)}, f32[768]{0:T(1024)S(1)}) all-reduce(f32[768]{0:T(1024)S(1)} %get-tuple-element.11, f32[768]{0:T(1024)S(1)} %convolution_reduce_fusion), channel_id=1, replica_groups=mesh['dp'=2,'rep'=4,'ind'=4] {'ind'}, use_global_device_ids=true, to_apply=%region_6.7 | all-reduce | flops 1536 | bytes 12288 | tf_op jit(solution)/shard_map/psum | solution.py:49
  198.1 1.3 subtract_reduce_fusion
  199.4 0.7 fusion.3
  200.1 12.9 %all-reduce = (f32[1024]{0:T(1024)S(1)}, f32[]{:T(128)}) all-reduce(f32[1024]{0:T(1024)S(1)} %bitcast.18, f32[]{:T(128)} %subtract_reduce_fusion), channel_id=1, replica_groups=mesh['dp'=2,'rep'=4,'ind'=4] {'dp','rep'}, use_global_device_ids=true, to_apply=%region_3.4 | all-reduce | flops 1025 | bytes 8200 | tf_op jit(solution)/shard_map/psum | solution.py:53
  213.0 0.0 copy-done.5
  213.0 1.2 divide_add_fusion
  214.3 86.0 %reduce-scatter.2.cloned.1.call-done = f32[1024,512]{1,0:T(8,128)} async-done(((f32[1024,4096]{1,0:T(8,128)}), f32[1024,512]{1,0:T(8,128)}) %reduce-scatter.2.cloned.1.call-update) | async-done | bytes 2097168 | tf_op jit(solution)/shard_map/reduce_scatter | solution.py:55
  300.3 6.4 %multiply_reduce_fusion.1 = (f32[]{:T(128)}, f32[1024,512]{1,0:T(8,128)}) fusion(f32[1024,512]{1,0:T(8,128)} %param.15, f32[1024,512]{1,0:T(8,128)} %reduce-scatter.2.cloned.1.call-done, f32[1024,512]{1,0:T(8,128)} %param.16, f32[]{:T(128)} %bitcast.2, s32[512]{0:T(512)S(1)} %iota_add_fusion.1, s32[1024]{0:T(1024)S(1)} %iota_add_fusion), kind=kLoop, calls=%fused_computation.2 | loop fusion | flops 4194303 | bytes 8394760 | tf_op jit(solution)/shard_map/reduce_sum | solution.py:57
  306.7 39.5 %psum.39 = f32[]{:T(128)} all-reduce(f32[]{:T(128)} %get-tuple-element.7), channel_id=1, replica_groups=mesh['dp'=2,'rep'=4,'ind'=4] {'dp','rep','ind'}, use_global_device_ids=true, to_apply=%region_10.11 | all-reduce | flops 1 | bytes 8 | tf_op jit(solution)/shard_map/psum | solution.py:57
  (11 shorter events, 0.1 us)
Async XLA Ops:
  7.2 180.8 %copy-start = (f32[1024]{0:T(1024)S(1)}, f32[1024]{0:T(1024)}, u32[]{:S(2)}) copy-start(f32[1024]{0:T(1024)} %param.14) | copy-start | bytes 12292
  7.2 30.6 %copy-start.2 = (f32[1024,64]{0,1:T(8,128)S(1)}, f32[1024,64]{0,1:T(8,128)}, u32[]{:S(2)}) copy-start(f32[1024,64]{0,1:T(8,128)} %param.12) | copy-start | bytes 786436
  7.2 165.7 %all-gather.2.cloned.1.call-start = ((), (), s32[]{:S(2)}) async-start(), calls=%async_computation.1 | async-start | bytes 7864320 | tf_op jit(solution)/shard_map/all_gather | solution.py:45
  7.2 11.6 %collective-permute-start = (f32[1024,64]{0,1:T(8,128)}, f32[1024,64]{0,1:T(8,128)S(1)}, u32[]{:S(2)}, u32[]{:S(2)}) collective-permute-start(f32[1024,64]{0,1:T(8,128)} %param.12), channel_id=1, source_target_pairs={{0,1},{1,2},{2,3},{3,0},{4,5},{5,6},{6,7},{7,4},{8,9},{9,10},{10,1... | collective-permute-start | bytes 786440 | tf_op jit(solution)/shard_map/ppermute | solution.py:34
  18.9 9.3 %collective-permute-start.1 = (f32[1024,64]{0,1:T(8,128)S(1)}, f32[1024,64]{0,1:T(8,128)S(1)}, u32[]{:S(2)}, u32[]{:S(2)}) collective-permute-start(f32[1024,64]{0,1:T(8,128)S(1)} %collective-permute-done), channel_id=1, source_target_pairs={{0,1},{1,2},{2,3},{3,0},{4,5},{5,6},{6,7},{7,4},{8,9},{9,10},{10,1... | collective-permute-start | bytes 786440 | tf_op jit(solution)/shard_map/ppermute | solution.py:34
  28.2 8.4 %collective-permute-start.2 = (f32[1024,64]{0,1:T(8,128)S(1)}, f32[1024,64]{0,1:T(8,128)S(1)}, u32[]{:S(2)}, u32[]{:S(2)}) collective-permute-start(f32[1024,64]{0,1:T(8,128)S(1)} %collective-permute-done.1), channel_id=1, source_target_pairs={{0,1},{1,2},{2,3},{3,0},{4,5},{5,6},{6,7},{7,4},{8,9},{9,10},{10,1... | collective-permute-start | bytes 786440 | tf_op jit(solution)/shard_map/ppermute | solution.py:34
  30.5 7.3 %copy-start.6 = (f32[64]{0:T(128)S(1)}, f32[64]{0:T(128)}, u32[]{:S(2)}) copy-start(f32[64]{0:T(128)} %param.18) | copy-start | bytes 772
  36.6 1.4 copy-start.3
  37.8 13.9 %slice-start = ((s8[8388608]{0:T(1024)(128)(4,1)}), s8[4194304]{0:T(1024)(128)(4,1)S(1)}, s32[]{:S(2)}) async-start(s8[8388608]{0:T(1024)(128)(4,1)} %bitcast.19), calls=%async_computation.3 | async-start | bytes 8388608
  38.0 13.6 %slice-start.1 = ((s8[8388608]{0:T(1024)(128)(4,1)}), s8[4194304]{0:T(1024)(128)(4,1)S(1)}, s32[]{:S(2)}) async-start(s8[8388608]{0:T(1024)(128)(4,1)} %bitcast.19), calls=%async_computation.4 | async-start | bytes 8388608
  59.5 113.3 %copy-start.1 = (bf16[768,1024]{1,0:T(8,128)(2,1)S(1)}, bf16[768,1024]{1,0:T(8,128)(2,1)}, u32[]{:S(2)}) copy-start(bf16[768,1024]{1,0:T(8,128)(2,1)} %get-tuple-element.12) | copy-start | bytes 4718596
  59.6 240.7 %reduce-scatter.2.cloned.1.call-start = ((), (), s32[]{:S(2)}) async-start(), calls=%async_computation.2 | async-start | bytes 18874368 | tf_op jit(solution)/shard_map/reduce_scatter | solution.py:55
  185.9 0.7 copy-start.4
  185.9 27.1 %copy-start.5 = (f32[1024]{0:T(1024)S(1)}, f32[1024]{0:T(1024)}, u32[]{:S(2)}) copy-start(f32[1024]{0:T(1024)} %param.17) | copy-start | bytes 12292
Sparse Core Ops, SparseCore 0:
  59.7 113.1 all-gather.1
  186.0 114.2 reduce-scatter.1
